TPU v7x, 32 devices: a whole 2x2x4 slice. The times are simulated.
32 devices in a mesh: blk: 8 (over y, x, core), ulysses: 4 (over z).
Axes of the slice: x: 2, y: 2, z: 4, core: 2. Of those that a mesh axis runs over, the one named last changes fastest.
Arguments:
- tokens: bfloat16 [2048, 3072], P(('blk', 'ulysses')), may hold values from -6 to 6
- mod_shift: float32 [3072], replicated, may hold values from -3 to 3
- mod_scale: float32 [3072], replicated, may hold values from -3 to 3
- mod_gate: float32 [3072], replicated, may hold values from 0.5 to 1.5
- qkv_weight: bfloat16 [3, 3072, 3072], P(None, None, 'ulysses'), may hold values from -0.109375 to 0.109375
- query_gain: float32 [128], replicated, may hold values from 1 to 16
- key_gain: float32 [128], replicated, may hold values from 1 to 16
- out_weight: bfloat16 [3072, 3072], P(None, 'ulysses'), may hold values from -0.109375 to 0.109375
Outputs:
- mixed: bfloat16 [2048, 3072], P(('blk', 'ulysses'))
All inputs are finite; a program needn't handle non-finite values.
Results may differ from a plain program's by a relative error of at most 0.013.
The roundings to bfloat16 on the way count: a program that leaves them out, or rounds other values in their place, can miss the bound.
Values may be sent and summed in bfloat16 or wider, within the bound.
No kernel may reach another device: no remote copies, remote signals or barrier semaphores. Data moves between devices by JAX's collectives and lax.ppermute only.
A program may use at most 128 MiB of HBM per device.

v0:
```python
import math
import jax
import jax.numpy as jnp
from jax import lax
from jax.sharding import PartitionSpec as P


def head_norm(projected, gain, factor):
    split = projected.reshape(projected.shape[0], -1, gain.shape[0])
    meansq = jnp.mean(split * split, axis=-1, keepdims=True)
    return (split * lax.rsqrt(meansq + 1e-06) * gain * factor).reshape(projected.shape)


def local(tokens, mod_shift, mod_scale, mod_gate, qkv_weight, query_gain, key_gain, out_weight):
    wide = tokens.astype(jnp.float32)
    center = jnp.mean(wide, axis=-1, keepdims=True)
    spread = jnp.mean((wide - center) ** 2, axis=-1, keepdims=True)
    normed = (wide - center) / jnp.sqrt(spread + 1e-06)
    modulated = (normed * (1.0 + mod_scale) + mod_shift).astype(jnp.bfloat16)
    head_size = query_gain.shape[0]
    local_width = qkv_weight.shape[2]
    heads_here = local_width // head_size
    factor = 1.0 / math.sqrt(head_size)
    sums = jnp.einsum(
        "rd,jde->jre",
        lax.all_gather(modulated, "ulysses", axis=0, tiled=True),
        qkv_weight,
        preferred_element_type=jnp.float32,
    )
    queries = head_norm(sums[0], query_gain, factor)
    keys = head_norm(sums[1], key_gain, 1.0)
    stacked = jnp.stack([queries, keys, sums[2]]).astype(jnp.bfloat16)
    queries, keys, values = (stacked[0], stacked[1], stacked[2])
    query_rows = queries.shape[0]
    query_heads = queries.reshape(query_rows, heads_here, head_size)
    start_state = (
        jnp.full((heads_here, query_rows), -1e30, jnp.float32),
        jnp.zeros((heads_here, query_rows), jnp.float32),
        jnp.zeros((heads_here, query_rows, head_size), jnp.float32),
    )
    key_part = lax.all_gather(keys, "blk", axis=0, tiled=True)
    value_part = lax.all_gather(values, "blk", axis=0, tiled=True)
    count = key_part.shape[0] // query_rows

    def step(position, state):
        highest, total, numerator = state
        key_block = lax.dynamic_slice_in_dim(key_part, position * query_rows, query_rows, 0)
        value_block = lax.dynamic_slice_in_dim(value_part, position * query_rows, query_rows, 0)
        key_block = key_block.reshape(query_rows, heads_here, head_size)
        value_block = value_block.reshape(query_rows, heads_here, head_size)
        scores = jnp.einsum(
            "qhd,khd->hqk", query_heads, key_block, preferred_element_type=jnp.float32
        )
        new_high = jnp.maximum(highest, jnp.max(scores, axis=-1))
        rescale = jnp.exp(highest - new_high)
        powers = jnp.exp(scores - new_high[..., None])
        total = total * rescale + jnp.sum(powers, axis=-1)
        numerator = numerator * rescale[..., None] + jnp.einsum(
            "hqk,khd->hqd",
            powers.astype(jnp.bfloat16),
            value_block,
            preferred_element_type=jnp.float32,
        )
        return (new_high, total, numerator)

    highest, total, numerator = lax.fori_loop(0, count, step, start_state)
    attended = (numerator / total[..., None]).transpose(1, 0, 2).reshape(query_rows, local_width)
    attended = attended.astype(jnp.bfloat16)
    columns = jnp.dot(
        lax.all_gather(attended, "ulysses", axis=1, tiled=True),
        out_weight,
        preferred_element_type=jnp.float32,
    )
    branch = lax.all_to_all(
        columns.astype(jnp.bfloat16), "ulysses", split_axis=0, concat_axis=1, tiled=True
    ).astype(columns.dtype)
    return (wide + mod_gate * branch).astype(jnp.bfloat16)


def solution(mesh):
    in_specs = (
        P(("blk", "ulysses"), None),
        P(),
        P(),
        P(),
        P(None, None, "ulysses"),
        P(),
        P(),
        P(None, "ulysses"),
    )
    out_specs = P(("blk", "ulysses"), None)
    return jax.shard_map(local, mesh=mesh, in_specs=in_specs, out_specs=out_specs, check_vma=False)
```

profile of v0, /device:TPU:0, one launch (start us, length us, event | category | flops | bytes accessed | tf_op | source)
XLA Modules:
  0.0 214.0 jit_solution(12685129563109106059)
XLA Ops:
  6.5 1.1 convert_reduce_fusion
  7.7 1.3 fusion.9
  9.0 0.7 broadcast_add_fusion
  9.7 2.0 fusion.12
  11.8 39.8 %all-gather.7.cloned.1.call-done = bf16[256,3072]{1,0:T(8,128)(2,1)} async-done(((bf16[64,3072]{1,0:T(8,128)(2,1)}), bf16[256,3072]{1,0:T(8,128)(2,1)}) %all-gather.7.cloned.1.call-update) | async-done | bytes 1572880 | tf_op jit(solution)/shard_map/all_gather | solution.py:26
  51.6 7.9 %convolution_bitcast_fusion = f32[3,256,768]{2,1,0:T(8,128)S(1)} fusion(bf16[3,3072,768]{2,1,0:T(8,128)(2,1)} %param.14, bf16[256,3072]{1,0:T(8,128)(2,1)} %all-gather.7.cloned.1.call-done), kind=kOutput, calls=%fused_computation.14 | convolution fusion | flops 3623878656 | bytes 18087936 | tf_op jit(solution)/shard_map/rd,jde->jre/dot_general | solution.py:24
  59.5 0.8 slice.32
  60.3 1.2 slice_multiply_fusion
  61.6 1.4 copy.30
  63.1 1.2 copy.31
  64.3 1.4 copy.28
  65.9 1.1 copy.29
  67.0 2.4 %multiply_convert_fusion = (bf16[1,256,768]{2,1,0:T(8,128)(2,1)S(1)}, bf16[1,256,768]{2,1,0:T(8,128)(2,1)}) fusion(f32[1,256,768]{2,1,0:T(8,128)} %copy.31, f32[3,256,768]{2,1,0:T(8,128)S(1)} %convolution_bitcast_fusion, f32[768]{0:T(1024)S(1)} %get-tuple-element.201, f32[768]{0:T(1024)S(1)} %get-tuple-element.202, f32[1,256,768]{2,1,0:T(8,128)} %copy.29), kind=kLoop, calls=%fused_computation.30 | loop fusion | flops 1376256 | bytes 3938304 | tf_op jit(solution)/shard_map/slice | solution.py:33
  69.9 21.6 %all-gather.13.cloned.1.call-done = bf16[1,2048,768]{2,1,0:T(8,128)(2,1)} async-done(((bf16[1,256,768]{2,1,0:T(8,128)(2,1)}), bf16[1,2048,768]{2,1,0:T(8,128)(2,1)}) %all-gather.13.cloned.1.call-update) | async-done | bytes 3145744 | tf_op jit(solution)/shard_map/all_gather | solution.py:42
  91.5 34.1 %all-gather.11.cloned.1.call-done = bf16[1,2048,768]{2,1,0:T(8,128)(2,1)} async-done(((bf16[1,256,768]{2,1,0:T(8,128)(2,1)}), bf16[1,2048,768]{2,1,0:T(8,128)(2,1)}) %all-gather.11.cloned.1.call-update) | async-done | bytes 3145744 | tf_op jit(solution)/shard_map/all_gather | solution.py:41
  125.6 23.6 %while.18 = (s32[]{:T(128)}, f32[6,256]{1,0:T(8,128)S(1)}, f32[6,256]{1,0:T(8,128)S(1)}, f32[6,256,128]{2,1,0:T(8,128)S(1)}, bf16[2048,768]{1,0:T(8,128)(2,1)}, ...) while((s32[]{:T(128)}, f32[6,256]{1,0:T(8,128)S(1)}, ...), condition=%wide.region_7.0_spmd.clone, body=%wide.region_4.0_spmd.clone.sunk | while | flops 203890176 | bytes 10715315 | solution.py:66
  125.6 1.2 constant_dynamic-slice_fusion.3
  127.1 0.4 bitcast_reduce_fusion.2
  127.8 0.7 convolution_add_fusion.2
  128.5 1.2 constant_dynamic-slice_fusion.3
  130.0 0.4 bitcast_reduce_fusion.2
  130.5 0.2 fusion.30
  130.7 0.7 convolution_add_fusion.2
  131.5 1.2 constant_dynamic-slice_fusion.3
  133.0 0.4 bitcast_reduce_fusion.2
  133.7 0.7 convolution_add_fusion.2
  134.4 1.2 constant_dynamic-slice_fusion.3
  135.9 0.4 bitcast_reduce_fusion.2
  136.6 0.7 convolution_add_fusion.2
  137.4 1.2 constant_dynamic-slice_fusion.3
  138.9 0.4 bitcast_reduce_fusion.2
  139.6 0.7 convolution_add_fusion.2
  140.3 1.2 constant_dynamic-slice_fusion.3
  141.8 0.4 bitcast_reduce_fusion.2
  142.5 0.7 convolution_add_fusion.2
  143.3 1.2 constant_dynamic-slice_fusion.3
  144.8 0.4 bitcast_reduce_fusion.2
  145.5 0.7 convolution_add_fusion.2
  146.2 1.2 constant_dynamic-slice_fusion.3
  147.7 0.4 bitcast_reduce_fusion.2
  148.4 0.7 convolution_add_fusion.2
  149.1 0.3 copy.36
  149.4 0.8 divide_convert_fusion
  150.2 37.2 %all-gather.9.cloned.1.call-done = bf16[256,3072]{0,1:T(8,128)(2,1)} async-done(((bf16[256,768]{0,1:T(8,128)(2,1)}), bf16[256,3072]{0,1:T(8,128)(2,1)}) %all-gather.9.cloned.1.call-update) | async-done | bytes 1572880 | tf_op jit(solution)/shard_map/all_gather | solution.py:70
  187.4 4.2 %convolution_convert_fusion = bf16[256,768]{1,0:T(8,128)(2,1)S(1)} fusion(bf16[256,3072]{0,1:T(8,128)(2,1)} %all-gather.9.cloned.1.call-done, bf16[3072,768]{1,0:T(8,128)(2,1)} %param.17), kind=kOutput, calls=%fused_computation.16 | convolution fusion | flops 1208156160 | bytes 6684672 | tf_op jit(solution)/shard_map/dot_general | solution.py:69
  191.7 13.9 %all_to_all.13 = bf16[4,64,768]{2,1,0:T(8,128)(2,1)S(1)} all-to-all(bf16[4,64,768]{2,1,0:T(8,128)(2,1)S(1)} %bitcast.69), channel_id=1, replica_groups=mesh['blk'=8,'ulysses'=4] {'ulysses'}, dimensions={0} | all-to-all | bytes 786432 | tf_op jit(solution)/shard_map/all_to_all | solution.py:74
  205.7 0.9 copy-done
  206.6 0.8 fusion.13
  (78 shorter events, 5.4 us)
Async XLA Ops:
  6.5 45.1 %all-gather.7.cloned.1.call-start = ((), (), s32[]{:S(2)}) async-start(), calls=%async_computation.1 | async-start | bytes 1966080 | tf_op jit(solution)/shard_map/all_gather | solution.py:26
  11.7 48.6 %copy-start.2 = (f32[128]{0:T(128)S(1)}, f32[128]{0:T(128)}, u32[]{:S(2)}) copy-start(f32[128]{0:T(128)} %param.15) | copy-start | bytes 1540
  11.7 48.6 %copy-start.3 = (f32[128]{0:T(128)S(1)}, f32[128]{0:T(128)}, u32[]{:S(2)}) copy-start(f32[128]{0:T(128)} %param.16) | copy-start | bytes 1540
  11.7 79.8 %all-gather.13.cloned.1.call-start = ((), (), s32[]{:S(2)}) async-start(), calls=%async_computation.4 | async-start | bytes 3538944 | tf_op jit(solution)/shard_map/all_gather | solution.py:42
  60.3 65.3 %all-gather.11.cloned.1.call-start = ((), (), s32[]{:S(2)}) async-start(), calls=%async_computation.3 | async-start | bytes 3538944 | tf_op jit(solution)/shard_map/all_gather | solution.py:41
  69.4 118.0 %all-gather.9.cloned.1.call-start = ((), (), s32[]{:S(2)}) async-start(), calls=%async_computation.2 | async-start | bytes 1966080 | tf_op jit(solution)/shard_map/all_gather | solution.py:70
  205.6 1.0 copy-start
  205.6 1.0 copy-start.1
Sparse Core Ops, SparseCore 0:
  11.8 39.7 all-gather.6
  60.4 31.0 all-gather.12
  93.4 32.1 all-gather.10
  150.4 37.0 all-gather.8
where the time goes:
time: 215 us; the launch traced here: 214 us
  waiting for transfers between devices  133 us (62%)
  matrix products  21 us (10%)
  local copies, waits for them, and re-layouts  19.7 us (9%)
  blocking collectives  13.9 us (6%)
  between operations  13.3 us (6%)
  other arithmetic  12.5 us (6%)
    all_gather x1, waiting for transfers between devices, local(): lax.all_gather(modulated, 'ulysses', axis=0, tiled=True)  39.8 us
    all_gather x1, waiting for transfers between devices, local(): lax.all_gather(attended, 'ulysses', axis=1, tiled=True)  37.2 us
    all_gather x1, waiting for transfers between devices, local(): key_part = lax.all_gather(keys, 'blk', axis=0, tiled=True)  34.1 us
    all_gather x1, waiting for transfers between devices, local(): value_part = lax.all_gather(values, 'blk', axis=0, tiled=True)  21.6 us
    all_to_all x1, blocking collectives, local(): lax.all_to_all(columns.astype(jnp.bfloat16), 'ulysses', split_axis=0, con...  13.9 us
    dynamic_slice x16, local copies, waits for them, and re-layouts, step(): lax.dynamic_slice_in_dim(value_part, position * query_rows, query_rows, 0)  10.7 us
    dot_general x1, matrix products, local(): jnp.einsum('rd,jde->jre', lax.all_gather(modulated, 'ulysses', axis=0, ti...  7.86 us
    dot_general x8, matrix products, step(): jnp.einsum('hqk,khd->hqd', powers.astype(jnp.bfloat16), value_block, pref...  5.52 us
  transfers between devices with their start and end apart: 4, of which 4 were waited for; matrix products, arithmetic and copies ran while one was open for 4% of the time, Pallas kernels for 0%

commit v1 on v0

--- a/solution.py
+++ b/solution.py
@@ -3,6 +3,12 @@
 import jax.numpy as jnp
 from jax import lax
 from jax.sharding import PartitionSpec as P
+
+
+def in_order(parts, dim):
+    parts = jnp.moveaxis(parts, 0, dim)
+    lengths = parts.shape
+    return parts.reshape(*lengths[:dim], lengths[dim] * lengths[dim + 1], *lengths[dim + 2 :])
 
 
 def head_norm(projected, gain, factor):
@@ -21,12 +27,18 @@
     local_width = qkv_weight.shape[2]
     heads_here = local_width // head_size
     factor = 1.0 / math.sqrt(head_size)
-    sums = jnp.einsum(
-        "rd,jde->jre",
-        lax.all_gather(modulated, "ulysses", axis=0, tiled=True),
-        qkv_weight,
-        preferred_element_type=jnp.float32,
-    )
+    size, here, extent = (lax.axis_size("ulysses"), lax.axis_index("ulysses"), modulated.shape[0])
+    right = [(i, (i + 1) % size) for i in range(size)]
+    blocks = []
+    carried = modulated
+    for turn in range(size):
+        coming = carried if turn == size - 1 else lax.ppermute(carried, "ulysses", right)
+        blocks.append(
+            jnp.einsum("rd,jde->jre", carried, qkv_weight, preferred_element_type=jnp.float32)
+        )
+        carried = coming
+    blocks = jnp.stack(blocks)[(here - jnp.arange(size)) % size]
+    sums = in_order(blocks, 1)
     queries = head_norm(sums[0], query_gain, factor)
     keys = head_norm(sums[1], key_gain, 1.0)
     stacked = jnp.stack([queries, keys, sums[2]]).astype(jnp.bfloat16)

time: 215 us -> 206 us (0.958)
  waiting for transfers between devices: 133 us -> 107 us
  matrix products: 21 us -> 38.5 us
  local copies, waits for them, and re-layouts: 19.7 us -> 16.1 us
  starting transfers between devices: 0.13 us -> 3.38 us
    all_gather x1 -> x0, waiting for transfers between devices: 39.8 us -> none  [local(): lax.all_gather(modulated, 'ulysses', axis=0, tiled=True)]
    dot_general x1 -> x4, matrix products: 7.86 us -> 25.4 us  [local(): jnp.einsum('rd,jde->jre', carried, qkv_weight, preferred_element_type=jnp...]
    ppermute x0 -> x3, waiting for transfers between devices: none -> 11.5 us  [local(): lax.ppermute(carried, 'ulysses', right)]
    ppermute x0 -> x3, starting transfers between devices: none -> 3.11 us  [local(): lax.ppermute(carried, 'ulysses', right)]
    mul x2, local copies, waits for them, and re-layouts: 2.79 us -> 0.24 us  [head_norm(): meansq = jnp.mean(split * split, axis=-1, keepdims=True)]
    mul x5 -> x2, local copies, waits for them, and re-layouts: 2.42 us -> 0.01 us  [head_norm(): split * lax.rsqrt(meansq + 1e-06) * gain * factor]
    gather x0 -> x1, local copies, waits for them, and re-layouts: none -> 2.18 us  [local(): blocks = jnp.stack(blocks)[(here - jnp.arange(size)) % size]]
    dynamic_slice x16 -> x8, local copies, waits for them, and re-layouts: 10.7 us -> 9.42 us  [step(): lax.dynamic_slice_in_dim(value_part, position * query_rows, query_rows, 0)]
  transfers between devices with their start and end apart: 4 -> 6, of which waited for: 4 -> 6; matrix products, arithmetic and copies ran while one was open for 4% -> 14% of each run, Pallas kernels for 0% -> 0%
where the time goes in v1:
time: 206 us
  waiting for transfers between devices  107 us (52%)
  matrix products  38.5 us (19%)
  local copies, waits for them, and re-layouts  16.1 us (8%)
  blocking collectives  14.1 us (7%)
  between operations  13.4 us (7%)
  other arithmetic  12.9 us (6%)
  starting transfers between devices  3.38 us (2%)
    all_gather x1, waiting for transfers between devices, local(): lax.all_gather(attended, 'ulysses', axis=1, tiled=True)  37.2 us
    all_gather x1, waiting for transfers between devices, local(): key_part = lax.all_gather(keys, 'blk', axis=0, tiled=True)  34.6 us
    dot_general x4, matrix products, local(): jnp.einsum('rd,jde->jre', carried, qkv_weight, preferred_element_type=jnp...  25.4 us
    all_gather x1, waiting for transfers between devices, local(): value_part = lax.all_gather(values, 'blk', axis=0, tiled=True)  23.5 us
    all_to_all x1, blocking collectives, local(): lax.all_to_all(columns.astype(jnp.bfloat16), 'ulysses', split_axis=0, con...  14.1 us
    ppermute x3, waiting for transfers between devices, local(): lax.ppermute(carried, 'ulysses', right)  11.5 us
    dynamic_slice x8, local copies, waits for them, and re-layouts, step(): lax.dynamic_slice_in_dim(value_part, position * query_rows, query_rows, 0)  9.42 us
    dot_general x8, matrix products, step(): jnp.einsum('hqk,khd->hqd', powers.astype(jnp.bfloat16), value_block, pref...  5.48 us
  transfers between devices with their start and end apart: 6, of which 6 were waited for; matrix products, arithmetic and copies ran while one was open for 14% of the time, Pallas kernels for 0%

profile of v1, /device:TPU:0, one launch (start us, length us, event | category | flops | bytes accessed | tf_op | source)
XLA Modules:
  0.0 205.8 jit_solution(5974549184022640450)
XLA Ops:
  6.5 1.2 convert_reduce_fusion
  7.7 1.3 fusion.8
  9.0 0.7 broadcast_add_fusion
  9.7 1.2 fusion.11
  10.9 3.1 %collective-permute-start = (bf16[64,3072]{1,0:T(8,128)(2,1)S(1)}, bf16[64,3072]{1,0:T(8,128)(2,1)S(1)}, u32[]{:S(2)}, u32[]{:S(2)}) collective-permute-start(bf16[64,3072]{1,0:T(8,128)(2,1)S(1)} %fusion.11), channel_id=1, source_target_pairs={{0,1},{1,2},{2,3},{3,0},{4,5},{5,6},{6,7},{7,4},{8,9},{9,10},{10,1... | collective-permute-start | bytes 1179656 | tf_op jit(solution)/shard_map/ppermute | solution.py:35
  14.0 7.6 %convolution_bitcast_fusion.3 = f32[1,3,64,768]{3,2,1,0:T(8,128)S(1)} fusion(bf16[3,3072,768]{2,1,0:T(8,128)(2,1)} %param.14, bf16[64,3072]{1,0:T(8,128)(2,1)S(1)} %fusion.11), kind=kOutput, calls=%fused_computation.20 | convolution fusion | flops 905969664 | bytes 15138816 | tf_op jit(solution)/shard_map/rd,jde->jre/dot_general | solution.py:37
  21.6 3.5 %collective-permute-done = bf16[64,3072]{1,0:T(8,128)(2,1)S(1)} collective-permute-done((bf16[64,3072]{1,0:T(8,128)(2,1)S(1)}, bf16[64,3072]{1,0:T(8,128)(2,1)S(1)}, u32[]{:S(2)}, u32[]{:S(2)}) %collective-permute-start) | collective-permute-done | bytes 393248 | tf_op jit(solution)/shard_map/ppermute | solution.py:35
  25.2 7.7 %convolution_bitcast_fusion.2 = f32[1,3,64,768]{3,2,1,0:T(8,128)S(1)} fusion(bf16[3,3072,768]{2,1,0:T(8,128)(2,1)} %param.14, bf16[64,3072]{1,0:T(8,128)(2,1)S(1)} %collective-permute-done), kind=kOutput, calls=%fused_computation.19 | convolution fusion | flops 905969664 | bytes 15138816 | tf_op jit(solution)/shard_map/rd,jde->jre/dot_general | solution.py:37
  32.9 4.3 %collective-permute-done.1 = bf16[64,3072]{1,0:T(8,128)(2,1)S(1)} collective-permute-done((bf16[64,3072]{1,0:T(8,128)(2,1)S(1)}, bf16[64,3072]{1,0:T(8,128)(2,1)S(1)}, u32[]{:S(2)}, u32[]{:S(2)}) %collective-permute-start.1) | collective-permute-done | bytes 393248 | tf_op jit(solution)/shard_map/ppermute | solution.py:35
  37.3 7.6 %convolution_bitcast_fusion.1 = f32[1,3,64,768]{3,2,1,0:T(8,128)S(1)} fusion(bf16[3,3072,768]{2,1,0:T(8,128)(2,1)} %param.14, bf16[64,3072]{1,0:T(8,128)(2,1)S(1)} %collective-permute-done.1), kind=kOutput, calls=%fused_computation.18 | convolution fusion | flops 905969664 | bytes 15138816 | tf_op jit(solution)/shard_map/rd,jde->jre/dot_general | solution.py:37
  44.8 3.7 %collective-permute-done.2 = bf16[64,3072]{1,0:T(8,128)(2,1)S(1)} collective-permute-done((bf16[64,3072]{1,0:T(8,128)(2,1)S(1)}, bf16[64,3072]{1,0:T(8,128)(2,1)S(1)}, u32[]{:S(2)}, u32[]{:S(2)}) %collective-permute-start.2) | collective-permute-done | bytes 393248 | tf_op jit(solution)/shard_map/ppermute | solution.py:35
  48.5 2.5 %convolution_bitcast_fusion = f32[1,3,64,768]{3,2,1,0:T(8,128)S(1)} fusion(bf16[3,3072,768]{2,1,0:T(8,128)(2,1)S(1)} %bitcast.108, bf16[64,3072]{1,0:T(8,128)(2,1)S(1)} %collective-permute-done.2), kind=kOutput, calls=%fused_computation.17 | convolution fusion | flops 905969664 | bytes 15138816 | tf_op jit(solution)/shard_map/rd,jde->jre/dot_general | solution.py:37
  51.3 2.2 %gather_fusion = f32[4,3,64,768]{3,2,1,0:T(8,128)} fusion(f32[4,3,64,768]{3,2,1,0:T(8,128)S(1)} %pad_maximum_fusion, s32[1024]{0:T(1024)S(1)} %pad_clamp_fusion), kind=kCustom, calls=%fused_computation | custom fusion | bytes 4718608 | tf_op jit(solution)/shard_map/gather | solution.py:40
  53.4 1.2 slice.35
  54.6 0.9 copy.38
  55.7 1.7 slice_multiply_fusion
  57.3 1.2 copy.35
  59.1 2.1 %fusion.17 = bf16[1,256,768]{1,2,0:T(8,128)(2,1)} fusion(f32[1,256,768]{1,2,0:T(8,128)} %copy.35, f32[768]{0:T(1024)S(1)} %broadcast_bitcast_fusion.1, f32[256,6]{0,1:T(8,128)S(1)} %add_rsqrt_fusion.1), kind=kLoop, calls=%fused_computation.38 | loop fusion | flops 589824 | bytes 1188864 | tf_op jit(solution)/shard_map/slice | solution.py:45
  62.7 23.5 %all-gather.5.cloned.1.call-done = bf16[2048,768]{0,1:T(8,128)(2,1)} async-done(((bf16[256,768]{0,1:T(8,128)(2,1)}), bf16[2048,768]{0,1:T(8,128)(2,1)}) %all-gather.5.cloned.1.call-update) | async-done | bytes 3145744 | tf_op jit(solution)/shard_map/all_gather | solution.py:54
  86.3 34.6 %all-gather.9.cloned.1.call-done = bf16[1,2048,768]{1,2,0:T(8,128)(2,1)} async-done(((bf16[1,256,768]{1,2,0:T(8,128)(2,1)}), bf16[1,2048,768]{1,2,0:T(8,128)(2,1)}) %all-gather.9.cloned.1.call-update) | async-done | bytes 3145744 | tf_op jit(solution)/shard_map/all_gather | solution.py:53
  120.9 20.8 %while.18 = (s32[]{:T(128)}, f32[6,256]{1,0:T(8,128)S(1)}, f32[6,256]{1,0:T(8,128)S(1)}, f32[6,256,128]{2,1,0:T(8,128)S(1)}, bf16[2048,768]{0,1:T(8,128)(2,1)}, ...) while((s32[]{:T(128)}, f32[6,256]{1,0:T(8,128)S(1)}, ...), condition=%wide.region_7.8_spmd.clone, body=%wide.region_4.7_spmd.clone.sunk | while | flops 203890176 | bytes 9142451 | solution.py:78
  120.9 1.2 constant_dynamic-slice_fusion.3
  122.1 0.4 bitcast_reduce_fusion.2
  122.8 0.7 convolution_add_fusion.2
  123.5 1.2 constant_dynamic-slice_fusion.3
  125.4 0.7 convolution_add_fusion.2
  126.1 1.2 constant_dynamic-slice_fusion.3
  127.3 0.4 bitcast_reduce_fusion.2
  128.0 0.7 convolution_add_fusion.2
  128.7 1.2 constant_dynamic-slice_fusion.3
  129.9 0.4 bitcast_reduce_fusion.2
  130.6 0.7 convolution_add_fusion.2
  131.3 1.2 constant_dynamic-slice_fusion.3
  132.5 0.4 bitcast_reduce_fusion.2
  133.2 0.7 convolution_add_fusion.2
  133.9 1.2 constant_dynamic-slice_fusion.3
  135.1 0.4 bitcast_reduce_fusion.2
  135.8 0.7 convolution_add_fusion.2
  136.5 1.2 constant_dynamic-slice_fusion.3
  137.7 0.4 bitcast_reduce_fusion.2
  138.4 0.7 convolution_add_fusion.2
  139.1 1.2 constant_dynamic-slice_fusion.3
  141.0 0.7 convolution_add_fusion.2
  141.9 0.8 divide_convert_fusion
  142.8 37.2 %all-gather.7.cloned.1.call-done = bf16[256,3072]{0,1:T(8,128)(2,1)} async-done(((bf16[256,768]{0,1:T(8,128)(2,1)}), bf16[256,3072]{0,1:T(8,128)(2,1)}) %all-gather.7.cloned.1.call-update) | async-done | bytes 1572880 | tf_op jit(solution)/shard_map/all_gather | solution.py:82
  180.0 4.2 %convolution_convert_fusion = bf16[256,768]{1,0:T(8,128)(2,1)S(1)} fusion(bf16[256,3072]{0,1:T(8,128)(2,1)} %all-gather.7.cloned.1.call-done, bf16[3072,768]{1,0:T(8,128)(2,1)} %param.17), kind=kOutput, calls=%fused_computation.16 | convolution fusion | flops 1208156160 | bytes 6684672 | tf_op jit(solution)/shard_map/dot_general | solution.py:81
  184.2 14.1 %all_to_all.13 = bf16[4,64,768]{2,1,0:T(8,128)(2,1)S(1)} all-to-all(bf16[4,64,768]{2,1,0:T(8,128)(2,1)S(1)} %bitcast.120), channel_id=1, replica_groups=mesh['blk'=8,'ulysses'=4] {'ulysses'}, dimensions={0} | all-to-all | bytes 786432 | tf_op jit(solution)/shard_map/all_to_all | solution.py:86
  198.4 0.8 fusion.12
  (83 shorter events, 5.6 us)
Async XLA Ops:
  6.5 49.1 %copy-start = (f32[128]{0:T(128)S(1)}, f32[128]{0:T(128)}, u32[]{:S(2)}) copy-start(f32[128]{0:T(128)} %param.16) | copy-start | bytes 1540
  6.5 79.7 %all-gather.5.cloned.1.call-start = ((), (), s32[]{:S(2)}) async-start(), calls=%async_computation.1 | async-start | bytes 3538944 | tf_op jit(solution)/shard_map/all_gather | solution.py:54
  10.9 14.2 %collective-permute-start = (bf16[64,3072]{1,0:T(8,128)(2,1)S(1)}, bf16[64,3072]{1,0:T(8,128)(2,1)S(1)}, u32[]{:S(2)}, u32[]{:S(2)}) collective-permute-start(bf16[64,3072]{1,0:T(8,128)(2,1)S(1)} %fusion.11), channel_id=1, source_target_pairs={{0,1},{1,2},{2,3},{3,0},{4,5},{5,6},{6,7},{7,4},{8,9},{9,10},{10,1... | collective-permute-start | bytes 1179656 | tf_op jit(solution)/shard_map/ppermute | solution.py:35
  25.2 12.1 %collective-permute-start.1 = (bf16[64,3072]{1,0:T(8,128)(2,1)S(1)}, bf16[64,3072]{1,0:T(8,128)(2,1)S(1)}, u32[]{:S(2)}, u32[]{:S(2)}) collective-permute-start(bf16[64,3072]{1,0:T(8,128)(2,1)S(1)} %collective-permute-done), channel_id=1, source_target_pairs={{0,1},{1,2},{2,3},{3,0},{4,5},{5,6},{6,7},{7,4},{8,9},{9,10},{10,1... | collective-permute-start | bytes 1179656 | tf_op jit(solution)/shard_map/ppermute | solution.py:35
  25.2 23.3 %slice-start = ((s8[14155776]{0:T(1024)(128)(4,1)}), s8[4194304]{0:T(1024)(128)(4,1)S(1)}, s32[]{:S(2)}) async-start(s8[14155776]{0:T(1024)(128)(4,1)} %bitcast.107), calls=%async_computation.4 | async-start | bytes 8388608
  25.2 23.3 %slice-start.1 = ((s8[14155776]{0:T(1024)(128)(4,1)}), s8[4194304]{0:T(1024)(128)(4,1)S(1)}, s32[]{:S(2)}) async-start(s8[14155776]{0:T(1024)(128)(4,1)} %bitcast.107), calls=%async_computation.5 | async-start | bytes 8388608
  32.9 15.6 %slice-start.2 = ((s8[14155776]{0:T(1024)(128)(4,1)}), s8[4194304]{0:T(1024)(128)(4,1)S(1)}, s32[]{:S(2)}) async-start(s8[14155776]{0:T(1024)(128)(4,1)} %bitcast.107), calls=%async_computation.6 | async-start | bytes 8388608
  32.9 15.6 %slice-start.3 = ((s8[14155776]{0:T(1024)(128)(4,1)}), s8[1572864]{0:T(1024)(128)(4,1)S(1)}, s32[]{:S(2)}) async-start(s8[14155776]{0:T(1024)(128)(4,1)} %bitcast.107), calls=%async_computation.7 | async-start | bytes 3145728
  37.3 11.2 %collective-permute-start.2 = (bf16[64,3072]{1,0:T(8,128)(2,1)S(1)}, bf16[64,3072]{1,0:T(8,128)(2,1)S(1)}, u32[]{:S(2)}, u32[]{:S(2)}) collective-permute-start(bf16[64,3072]{1,0:T(8,128)(2,1)S(1)} %collective-permute-done.1), channel_id=1, source_target_pairs={{0,1},{1,2},{2,3},{3,0},{4,5},{5,6},{6,7},{7,4},{8,9},{9,10},{10,1... | collective-permute-start | bytes 1179656 | tf_op jit(solution)/shard_map/ppermute | solution.py:35
  55.6 65.3 %all-gather.9.cloned.1.call-start = ((), (), s32[]{:S(2)}) async-start(), calls=%async_computation.3 | async-start | bytes 3538944 | tf_op jit(solution)/shard_map/all_gather | solution.py:53
  58.5 2.9 %copy-start.3 = (f32[128]{0:T(128)S(1)}, f32[128]{0:T(128)}, u32[]{:S(2)}) copy-start(f32[128]{0:T(128)} %param.15) | copy-start | bytes 1540
  61.2 118.8 %all-gather.7.cloned.1.call-start = ((), (), s32[]{:S(2)}) async-start(), calls=%async_computation.2 | async-start | bytes 1966080 | tf_op jit(solution)/shard_map/all_gather | solution.py:82
  184.2 14.2 %copy-start.1 = (bf16[64,3072]{1,0:T(8,128)(2,1)S(1)}, bf16[64,3072]{1,0:T(8,128)(2,1)}, u32[]{:S(2)}) copy-start(bf16[64,3072]{1,0:T(8,128)(2,1)} %param.10) | copy-start | bytes 1179652
  184.2 14.2 %copy-start.2 = (f32[3072]{0:T(1024)S(1)}, f32[3072]{0:T(1024)}, u32[]{:S(2)}) copy-start(f32[3072]{0:T(1024)} %param.13) | copy-start | bytes 36868
Sparse Core Ops, SparseCore 0:
  55.7 30.5 all-gather.4
  88.1 32.7 all-gather.8
  142.9 37.0 all-gather.6
